TPU v7x, 32 devices: a whole 2x2x4 slice. The times are simulated.
32 devices in a mesh: dom: 8 (over y, x, core), feat: 4 (over z).
Axes of the slice: x: 2, y: 2, z: 4, core: 2. Of those that a mesh axis runs over, the one named last changes fastest.
Arguments:
- features: bfloat16 [128, 131072], P('feat', 'dom'), may hold values from -6 to 6
- seed_rows: int32 [2048], P('dom'), may hold values from 0 to 16383
- want_rows: int32 [8, 8, 128], P('dom'), may hold values from 0 to 16383
- live_counts: int32 [8, 8], P('dom'), may hold values from 1 to 128, as said below
- hop_one: int32 [15, 2048], P(None, 'dom'), may hold values from 0 to 1023, as said below
- hop_two: int32 [10, 15, 2048], P(None, None, 'dom'), may hold values from 0 to 1023, as said below
- w1_self: bfloat16 [256, 128], replicated, may hold values from -0.5 to 0.5
- w1_neigh: bfloat16 [256, 128], replicated, may hold values from -0.5 to 0.5
- b1: float32 [256], P('feat'), may hold values from -4 to 4
- w2_self: bfloat16 [256, 256], P(None, 'feat'), may hold values from -0.375 to 0.375
- w2_neigh: bfloat16 [256, 256], P(None, 'feat'), may hold values from -0.375 to 0.375
- b2: float32 [256], P('feat'), may hold values from -4 to 4
Outputs:
- embed: float32 [256, 2048], P('feat', 'dom')
Inputs may be any that keep to these rules, and one draw needn't show every extreme that they name: `want_rows`: slots at or beyond live_counts[r, o] are ignored. `live_counts`: in every draw a quarter of the owners, every fourth one from a drawn offset, receive all 128 slots from every requester. `hop_one`: each entry is o * 128 + c, a position in the buffer of the requester that holds seed s, with c < live_counts of that requester and owner o. `hop_two`: each entry is o * 128 + c, a position in the buffer of the requester that holds seed s, with c < live_counts of that requester and owner o.
All inputs are finite; a program needn't handle non-finite values.
Results may differ from a plain program's by a relative error of at most 0.00036.
Values may be sent and summed in bfloat16 or wider, within the bound.
A program may use at most 64 MiB of HBM per device.

v0:
```python
import jax
import jax.numpy as jnp
from jax import lax
from jax.sharding import PartitionSpec as P

OUT = 256
FAN1 = 15
FAN2 = 10
CAP = 128


def aggregate_counts(fetched, hop_one, hop_two):
    feat_dev, slots = fetched.shape
    width = CAP * 4
    first = hop_one.reshape(1, -1)
    second = hop_two.reshape(FAN2, -1)
    columns = first.shape[1]

    def add_block(blocks, carry):
        start = blocks * width
        piece = lax.dynamic_slice_in_dim(fetched, start, width, 1)
        place = start + lax.broadcasted_iota(jnp.int32, (width, 1), 0)
        pick_one = (first == place).astype(jnp.bfloat16)
        pick_two = jnp.zeros((width, columns), jnp.bfloat16)
        for sample in range(FAN2):
            pick_two = pick_two + (second[sample : sample + 1] == place).astype(jnp.bfloat16)
        own_sum = carry[0] + jnp.dot(piece, pick_one, preferred_element_type=jnp.float32)
        mean_sum = carry[1] + jnp.dot(piece, pick_two, preferred_element_type=jnp.float32)
        return (own_sum, mean_sum)

    zeros = jnp.zeros((feat_dev, columns), jnp.float32)
    own_sum, mean_sum = lax.fori_loop(0, slots // width, add_block, (zeros, zeros))
    return (own_sum.astype(jnp.bfloat16), (mean_sum * (1.0 / FAN2)).astype(jnp.bfloat16))


def per_device(
    features,
    seed_rows,
    want_rows,
    live_counts,
    hop_one,
    hop_two,
    w1_self,
    w1_neigh,
    b1,
    w2_self,
    w2_neigh,
    b2,
):
    feat_dev = features.shape[0]
    seed_dev = seed_rows.shape[0]
    hid_dev = b1.shape[0]
    served = jnp.take(
        features,
        lax.all_to_all(want_rows, "dom", split_axis=1, concat_axis=0, tiled=True)[:, 0, :],
        axis=1,
    )
    returned = lax.all_to_all(served, "dom", split_axis=1, concat_axis=1, tiled=True)
    slot_ids = lax.broadcasted_iota(jnp.int32, (1, returned.shape[2]), 1)
    live_slots = slot_ids < live_counts[0][:, None]
    fetched = jnp.where(live_slots[None], returned, jnp.zeros((), jnp.bfloat16)).reshape(
        feat_dev, -1
    )
    x_one, m_two = aggregate_counts(fetched, hop_one, hop_two)
    x_seed = jnp.take(features, seed_rows, axis=1)
    m_one = jnp.sum(x_one.reshape(feat_dev, FAN1, seed_dev), axis=1, dtype=jnp.float32)
    m_one = (m_one * (1.0 / FAN1)).astype(jnp.bfloat16)
    selves = jnp.concatenate([x_one, x_seed], axis=1)
    means = jnp.concatenate([m_two, m_one], axis=1)
    hid_start = lax.axis_index("feat") * hid_dev
    self_rows = lax.dynamic_slice_in_dim(w1_self, hid_start, hid_dev, 0)
    neigh_rows = lax.dynamic_slice_in_dim(w1_neigh, hid_start, hid_dev, 0)
    self_part = self_rows
    neigh_part = neigh_rows
    total = jnp.dot(
        self_part,
        lax.all_gather(selves, "feat", axis=0, tiled=True),
        preferred_element_type=jnp.float32,
    )
    pre = total + jnp.dot(
        neigh_part,
        lax.all_gather(means, "feat", axis=0, tiled=True),
        preferred_element_type=jnp.float32,
    )
    hidden = jnp.maximum(pre + b1[:, None], 0.0)
    hop_cols = FAN1 * seed_dev
    h_one = hidden[:, :hop_cols]
    h_seed = hidden[:, hop_cols:]
    g_mean = jnp.sum(h_one.reshape(hid_dev, FAN1, seed_dev), axis=1) * (1.0 / FAN1)
    second_self = w2_self.astype(jnp.float32)
    second_neigh = w2_neigh.astype(jnp.float32)
    self_part = second_self
    neigh_part = second_neigh
    total = jnp.dot(
        self_part, h_seed, precision=lax.Precision.HIGHEST, preferred_element_type=jnp.float32
    )
    z_out = (
        lax.psum_scatter(
            total
            + jnp.dot(
                neigh_part,
                g_mean,
                precision=lax.Precision.HIGHEST,
                preferred_element_type=jnp.float32,
            ),
            "feat",
            scatter_dimension=0,
            tiled=True,
        )
        + b2[:, None]
    )
    square = lax.psum(jnp.sum(z_out * z_out, axis=0), "feat")
    return z_out * lax.rsqrt(square * (1.0 / OUT) + 1.0)


def solution(mesh):
    return jax.shard_map(
        per_device,
        mesh=mesh,
        in_specs=(
            P("feat", "dom"),
            P("dom"),
            P("dom", None, None),
            P("dom", None),
            P(None, "dom"),
            P(None, None, "dom"),
            P(),
            P(),
            P("feat"),
            P(None, "feat"),
            P(None, "feat"),
            P("feat"),
        ),
        out_specs=P("feat", "dom"),
        check_vma=False,
    )
```

profile of v0, /device:TPU:0, one launch (start us, length us, event | category | flops | bytes accessed | tf_op | source)
XLA Modules:
  0.0 154.3 jit_solution(16646595926999399263)
XLA Ops:
  6.5 5.3 %all-to-all-start = ((s32[1,8,128]{2,0,1:T(1,128)}), s32[1,8,128]{2,0,1:T(1,128)S(1)}, u32[]{:S(2)}, u32[]{:S(2)}) async-start(s32[1,8,128]{2,0,1:T(1,128)} %bitcast.38), calls=%async_computation | async-start | bytes 8192 | tf_op jit(solution)/shard_map/all_to_all | solution.py:55
  11.9 0.7 compare_select_fusion.2
  12.6 0.7 compare_and_fusion.1
  13.2 4.6 %copy.30 = bf16[32,16384]{0,1:T(8,128)(2,1)} copy(bf16[32,16384]{1,0:T(8,128)(2,1)} %param.14) | data formatting | bytes 2097152 | tf_op args[0]
  17.8 3.5 %gather_fusion.1 = bf16[256,32]{1,0:T(8,128)(2,1)S(1)} fusion(bf16[32,16384]{0,1:T(8,128)(2,1)} %copy.30, s32[1024]{0:T(1024)S(1)} %pad_clamp_fusion), kind=kCustom, calls=%fused_computation.1 | custom fusion | bytes 33792 | tf_op jit(solution)/shard_map/jit(_take)/gather | solution.py:65
  21.3 0.1 select_bitcast_fusion
  21.4 5.6 %gather_fusion = bf16[1024,32]{1,0:T(8,128)(2,1)S(1)} fusion(bf16[32,16384]{0,1:T(8,128)(2,1)} %copy.30, s32[1024]{0:T(1024)S(1)} %fusion.43), kind=kCustom, calls=%fused_computation | custom fusion | bytes 135168 | tf_op jit(solution)/shard_map/jit(_take)/gather | solution.py:53
  27.0 0.1 copy.31
  27.2 0.6 select_bitcast_fusion.1
  27.8 4.2 %all-to-all-start.1 = ((bf16[32,8,128]{2,0,1:T(8,128)(2,1)}), bf16[32,8,128]{2,0,1:T(8,128)(2,1)S(1)}, u32[]{:S(2)}, u32[]{:S(2)}) async-start(bf16[32,8,128]{2,0,1:T(8,128)(2,1)} %select_bitcast_fusion.1), calls=%async_computation.1 | async-start | bytes 131072 | tf_op jit(solution)/shard_map/all_to_all | solution.py:58
  32.0 0.2 all-gather.3.cloned.1.call-start
  32.3 0.1 iota_compare_fusion
  32.3 0.1 copy.34
  32.5 0.1 copy.40
  32.6 4.4 %all-to-all-done.1 = bf16[32,8,128]{2,0,1:T(8,128)(2,1)S(1)} async-done(((bf16[32,8,128]{2,0,1:T(8,128)(2,1)}), bf16[32,8,128]{2,0,1:T(8,128)(2,1)S(1)}, u32[]{:S(2)}, u32[]{:S(2)}) %all-to-all-start.1) | async-done | bytes 65568 | tf_op jit(solution)/shard_map/all_to_all | solution.py:58
  37.1 19.3 %while.16 = (s32[]{:T(128)}, f32[32,3840]{1,0:T(8,128)S(1)}, f32[32,3840]{1,0:T(8,128)S(1)}, bf16[32,1024]{1,0:T(8,128)(2,1)S(1)}, s32[1,3840]{1,0:T(1,128)S(1)}...) while((s32[]{:T(128)}, f32[32,3840]{1,0:T(8,128)S(1)}, ...), condition=%wide.region_1.2_spmd.clone, body=%wide.region_0.1_spmd.clone.sunk | while | flops 311132672 | bytes 2556086 | solution.py:32
  37.1 1.5 fusion.60
  38.6 0.4 slice_reduce_fusion.11
  39.0 7.7 %convolution_add_fusion.4 = f32[32,3840]{1,0:T(8,128)S(1)} fusion(s32[3840]{0:T(1024)S(1)} %get-tuple-element.207, s32[3840]{0:T(1024)S(1)} %get-tuple-element.208, s32[3840]{0:T(1024)S(1)} %get-tuple-element.209, s32[3840]{0:T(1024)S(1)} %get-tuple-element.210, s32[3840]{0:T(1024)S(1)} %get-tuple-element.211, s32[3840]{0:T(1024)S(1)} %get-tuple-element.212, ...), kind=kOutput, calls=%fused_computation.14.clone.1 | convolution fusion | flops 183091200 | bytes 1181701 | tf_op jit(solution)/shard_map/while/body/eval_jaxpr/dot_general | solution.py:28
  46.8 1.5 fusion.60
  48.3 0.4 slice_reduce_fusion.11
  48.7 7.7 %convolution_add_fusion.4 = f32[32,3840]{1,0:T(8,128)S(1)} fusion(s32[3840]{0:T(1024)S(1)} %get-tuple-element.207, s32[3840]{0:T(1024)S(1)} %get-tuple-element.208, s32[3840]{0:T(1024)S(1)} %get-tuple-element.209, s32[3840]{0:T(1024)S(1)} %get-tuple-element.210, s32[3840]{0:T(1024)S(1)} %get-tuple-element.211, s32[3840]{0:T(1024)S(1)} %get-tuple-element.212, ...), kind=kOutput, calls=%fused_computation.14.clone.1 | convolution fusion | flops 183091200 | bytes 1181701 | tf_op jit(solution)/shard_map/while/body/eval_jaxpr/dot_general | solution.py:28
  56.4 0.0 copy-start.6
  56.5 0.2 reshape.90
  56.7 0.7 pad_maximum_fusion
  57.4 0.0 all-gather.3.cloned.1.call-update
  57.4 0.0 all-gather.5.cloned.1.call-start
  57.5 0.1 reduce_sum.27
  57.7 0.7 pad_maximum_fusion.1
  58.4 0.0 all-gather.5.cloned.1.call-update
  58.4 0.0 reduce-scatter.4.cloned.1.call-start
  58.5 26.5 %all-gather.3.cloned.1.call-done = bf16[128,4096]{1,0:T(8,128)(2,1)} async-done(((bf16[32,4096]{1,0:T(8,128)(2,1)}), bf16[128,4096]{1,0:T(8,128)(2,1)}) %all-gather.3.cloned.1.call-update) | async-done | bytes 1048592 | tf_op jit(solution)/shard_map/all_gather | solution.py:77
  84.9 1.5 fusion.40
  86.5 27.4 %all-gather.5.cloned.1.call-done = bf16[128,4096]{1,0:T(8,128)(2,1)} async-done(((bf16[32,4096]{1,0:T(8,128)(2,1)}), bf16[128,4096]{1,0:T(8,128)(2,1)}) %all-gather.5.cloned.1.call-update) | async-done | bytes 1048592 | tf_op jit(solution)/shard_map/all_gather | solution.py:82
  113.9 1.5 fusion.33
  115.4 0.1 slice.93
  115.5 0.3 fusion.35
  115.9 0.3 reshape.89
  116.2 0.2 reduce_sum.28
  116.4 0.3 fusion.34
  116.7 0.8 copy.36
  117.5 0.0 reduce-scatter.4.cloned.1.call-update
  117.5 19.5 %reduce-scatter.4.cloned.1.call-done = f32[64,256]{1,0:T(8,128)} async-done(((f32[256,256]{1,0:T(8,128)}), f32[64,256]{1,0:T(8,128)}) %reduce-scatter.4.cloned.1.call-update) | async-done | bytes 65552
  137.1 0.9 copy.37
  138.0 0.1 multiply_reduce_fusion
  138.1 8.8 %psum.7 = f32[256]{0:T(256)S(1)} all-reduce(f32[256]{0:T(256)S(1)} %multiply_reduce_fusion), channel_id=1, replica_groups=mesh['dom'=8,'feat'=4] {'feat'}, use_global_device_ids=true, to_apply=%region_6.7 | all-reduce | flops 256 | bytes 2048 | tf_op jit(solution)/shard_map/psum | solution.py:112
  147.0 0.1 add_multiply_fusion
  147.1 0.7 copy.35
  (32 shorter events, 0.3 us)
Async XLA Ops:
  6.5 78.4 %copy-start = (bf16[256,128]{1,0:T(8,128)(2,1)S(1)}, bf16[256,128]{1,0:T(8,128)(2,1)}, u32[]{:S(2)}) copy-start(bf16[256,128]{1,0:T(8,128)(2,1)} %param.20) | copy-start | bytes 196612
  6.5 25.7 %copy-start.7 = (s32[1,8]{1,0:T(1,128)S(1)}, s32[1,8]{1,0:T(1,128)}, u32[]{:S(2)}) copy-start(s32[1,8]{1,0:T(1,128)} %param.17) | copy-start | bytes 100
  6.5 25.9 %copy-start.4 = (s32[15,256]{1,0:T(8,128)S(1)}, s32[15,256]{1,0:T(8,128)}, u32[]{:S(2)}) copy-start(s32[15,256]{1,0:T(8,128)} %param.18) | copy-start | bytes 46084
  6.5 25.9 %copy-start.1 = (s32[10,15,256]{2,1,0:T(8,128)S(1)}, s32[10,15,256]{2,1,0:T(8,128)}, u32[]{:S(2)}) copy-start(s32[10,15,256]{2,1,0:T(8,128)} %param.19) | copy-start | bytes 460804
  6.5 14.9 %all-to-all-start = ((s32[1,8,128]{2,0,1:T(1,128)}), s32[1,8,128]{2,0,1:T(1,128)S(1)}, u32[]{:S(2)}, u32[]{:S(2)}) async-start(s32[1,8,128]{2,0,1:T(1,128)} %bitcast.38), calls=%async_computation | async-start | bytes 8192 | tf_op jit(solution)/shard_map/all_to_all | solution.py:55
  27.8 9.2 %all-to-all-start.1 = ((bf16[32,8,128]{2,0,1:T(8,128)(2,1)}), bf16[32,8,128]{2,0,1:T(8,128)(2,1)S(1)}, u32[]{:S(2)}, u32[]{:S(2)}) async-start(bf16[32,8,128]{2,0,1:T(8,128)(2,1)} %select_bitcast_fusion.1), calls=%async_computation.1 | async-start | bytes 131072 | tf_op jit(solution)/shard_map/all_to_all | solution.py:58
  32.0 52.9 %all-gather.3.cloned.1.call-start = ((), (), s32[]{:S(2)}) async-start(), calls=%async_computation.3 | async-start | bytes 1310720 | tf_op jit(solution)/shard_map/all_gather | solution.py:77
  56.4 57.5 %copy-start.6 = (f32[64]{0:T(128)S(1)}, f32[64]{0:T(128)}, u32[]{:S(2)}) copy-start(f32[64]{0:T(128)} %param.22) | copy-start | bytes 772
  57.4 56.5 %all-gather.5.cloned.1.call-start = ((), (), s32[]{:S(2)}) async-start(), calls=%async_computation.4 | async-start | bytes 1310720 | tf_op jit(solution)/shard_map/all_gather | solution.py:82
  57.6 57.9 %copy-start.3 = (bf16[256,64]{0,1:T(8,128)(2,1)S(1)}, bf16[256,64]{0,1:T(8,128)(2,1)}, u32[]{:S(2)}) copy-start(bf16[256,64]{0,1:T(8,128)(2,1)} %param.23) | copy-start | bytes 98308
  58.4 78.7 %reduce-scatter.4.cloned.1.call-start = ((), (), s32[]{:S(2)}) async-start(), calls=%async_computation.5 | async-start | bytes 327680
  86.5 29.9 %copy-start.2 = (bf16[256,64]{0,1:T(8,128)(2,1)S(1)}, bf16[256,64]{0,1:T(8,128)(2,1)}, u32[]{:S(2)}) copy-start(bf16[256,64]{0,1:T(8,128)(2,1)} %param.24) | copy-start | bytes 98308
  115.4 22.6 %copy-start.5 = (f32[64]{0:T(128)S(1)}, f32[64]{0:T(128)}, u32[]{:S(2)}) copy-start(f32[64]{0:T(128)} %param.25) | copy-start | bytes 772
Sparse Core Ops, SparseCore 0:
  57.5 27.3 all-gather.2
  86.5 27.3 all-gather.4
  117.7 19.3 reduce-scatter.3
where the time goes:
time: 155 us; the launch traced here: 154 us
  waiting for transfers between devices  77.9 us (50%)
  matrix products  22 us (14%)
  local copies, waits for them, and re-layouts  17.9 us (12%)
  between operations  13.4 us (9%)
  starting transfers between devices  9.84 us (6%)
  blocking collectives  8.85 us (6%)
  other arithmetic  4.35 us (3%)
    all_gather x1, waiting for transfers between devices, per_device(): lax.all_gather(means, 'feat', axis=0, tiled=True)  27.4 us
    all_gather x1, waiting for transfers between devices, per_device(): lax.all_gather(selves, 'feat', axis=0, tiled=True)  26.5 us
    unnamed x4, waiting for transfers between devices  19.6 us
    dot_general x2, matrix products, add_block(): jnp.dot(piece, pick_two, preferred_element_type=jnp.float32)  15.4 us
    psum x1, blocking collectives, per_device(): square = lax.psum(jnp.sum(z_out * z_out, axis=0), 'feat')  8.85 us
    unnamed x22, local copies, waits for them, and re-layouts  6.56 us
    gather x2, local copies, waits for them, and re-layouts, per_device(): jnp.take(features, lax.all_to_all(want_rows, 'dom', split_axis=1, concat_...  5.73 us
    all_to_all x1, starting transfers between devices, per_device(): lax.all_to_all(want_rows, 'dom', split_axis=1, concat_axis=0, tiled=True)  5.34 us
  transfers between devices with their start and end apart: 5, of which 4 were waited for; matrix products, arithmetic and copies ran while one was open for 8% of the time, Pallas kernels for 0%

commit v1 on v0

v1 whole, which is shorter than its diff:
```python
import functools

import jax
import jax.numpy as jnp
from jax import lax
from jax.experimental import pallas as pl
from jax.experimental.pallas import tpu as pltpu
from jax.sharding import PartitionSpec as P

LANES = 128
MESH = pl.DeviceIdType.MESH
BF16 = jnp.bfloat16
F32 = jnp.float32


def gather_columns(feat_vm, rows):
    height, nodes = feat_vm.shape
    shape = (height, LANES)
    high = [jnp.broadcast_to(r >> 7, shape) for r in rows]
    low = [jnp.broadcast_to(r & (LANES - 1), shape) for r in rows]
    step = 4

    def body(i, accs):
        for u in range(step):
            t = i * step + u
            start = pl.multiple_of(t * LANES, LANES)
            tile = feat_vm[:, pl.ds(start, LANES)].astype(F32)
            accs = tuple(
                jnp.where(
                    h == t,
                    jnp.take_along_axis(tile, l, axis=1, mode="promise_in_bounds"),
                    a,
                )
                for a, h, l in zip(accs, high, low)
            )
        return accs

    init = tuple(jnp.zeros(shape, F32) for _ in rows)
    return lax.fori_loop(0, nodes // LANES // step, body, init)


def split_three(x):
    a = x.astype(BF16)
    rest = x - a.astype(F32)
    b = rest.astype(BF16)
    c = (rest - b.astype(F32)).astype(BF16)
    return a, b, c


def kernel(
    nd,
    nf,
    feat_hbm,
    seed_ref,
    want_ref,
    live_ref,
    one_ref,
    two_ref,
    w1s_ref,
    w1n_ref,
    w2_ref,
    bias_ref,
    out_ref,
    feat_vm,
    got,
    served,
    back,
    everyone,
    seed_own,
    seed_all,
    w2_all,
    bias_all,
    hop_rows,
    pick_one,
    pick_two,
    fetched,
    x_all,
    m_all,
    w2_full,
    z_own,
    z_all,
    local_sem,
    want_send,
    want_recv,
    serve_send,
    serve_recv,
    all_send,
    all_recv,
    seed_send,
    seed_recv,
    w2_send,
    w2_recv,
    bias_send,
    bias_recv,
    z_send,
    z_recv,
):
    height = feat_vm.shape[0]
    fan1, seeds = one_ref.shape
    fan2 = two_ref.shape[0]
    sub = seeds // nf
    per = LANES // sub
    chunks = (fan1 + 1) * sub // LANES
    hid_dev = out_ref.shape[0]
    hid = w1s_ref.shape[0]
    depth = w1s_ref.shape[1]
    me = lax.axis_index("dom")
    mf = lax.axis_index("feat")

    def dom_at(d):
        return lax.rem(me + d, nd)

    def feat_at(d):
        return lax.rem(mf + d, nf)

    feat_copy = pltpu.make_async_copy(feat_hbm, feat_vm, local_sem)
    feat_copy.start()

    barrier = pltpu.get_barrier_semaphore()
    for d in range(1, nd):
        pl.semaphore_signal(barrier, inc=1, device_id={"dom": dom_at(d)}, device_id_type=MESH)
    for d in range(1, nf):
        pl.semaphore_signal(barrier, inc=1, device_id={"feat": feat_at(d)}, device_id_type=MESH)
    pl.semaphore_wait(barrier, nd + nf - 2)

    def remote(src, dst, send, recv, where):
        copy = pltpu.make_async_remote_copy(
            src_ref=src,
            dst_ref=dst,
            send_sem=send,
            recv_sem=recv,
            device_id=where,
            device_id_type=MESH,
        )
        copy.start()
        return copy

    wants = [
        remote(want_ref.at[0], got.at[me], want_send.at[d], want_recv.at[d], {"dom": dom_at(d)})
        for d in range(1, nd)
    ]
    early = []
    for d in range(1, nf):
        where = {"feat": feat_at(d)}
        early.append(remote(bias_ref, bias_all.at[mf], bias_send.at[d], bias_recv.at[d], where))
        early.append(remote(w2_ref, w2_all.at[mf], w2_send.at[d], w2_recv.at[d], where))
    got[me] = want_ref[0]
    bias_all[mf] = bias_ref[...]
    w2_all[mf] = w2_ref[...]

    feat_copy.wait()
    groups = seeds // LANES
    for g, block in enumerate(
        gather_columns(feat_vm, [seed_ref[:, g * LANES : (g + 1) * LANES] for g in range(groups)])
    ):
        seed_own[g] = block.astype(BF16)
    seed_copies = [
        remote(
            seed_own.at[feat_at(d) * sub // LANES],
            seed_all.at[mf],
            seed_send.at[d],
            seed_recv.at[d],
            {"feat": feat_at(d)},
        )
        for d in range(1, nf)
    ]
    seed_all[mf] = seed_own[mf * sub // LANES]

    for copy in wants:
        copy.wait_recv()

    serves = []
    order = list(range(1, nd)) + [0]
    for first in range(0, nd, 4):
        part = order[first : first + 4]
        blocks = gather_columns(feat_vm, [got[dom_at(d), pl.ds(me, 1), :] for d in part])
        for d, block in zip(part, blocks):
            if d == 0:
                back[me] = block.astype(BF16)
                continue
            served[d] = block.astype(BF16)
            serves.append(
                remote(
                    served.at[d],
                    back.at[me],
                    serve_send.at[d],
                    serve_recv.at[d],
                    {"dom": dom_at(d)},
                )
            )

    lane = lax.broadcasted_iota(jnp.int32, (1, LANES), 1)
    base = pl.multiple_of(mf * sub // LANES * LANES, LANES)
    within = lax.rem(mf * sub, LANES)
    for k in range(fan2 + 1):
        if k < fan2:
            rows = two_ref[k, :, pl.ds(base, LANES)]
        else:
            rows = one_ref[:, pl.ds(base, LANES)]
        turned = [
            pltpu.roll(rows, lax.rem(q * sub - within + LANES, LANES), 1) for q in range(per)
        ]
        for c in range(chunks):
            row = jnp.full((1, LANES), -1, jnp.int32)
            for q in range(per):
                j = c * per + q
                if j < fan1:
                    inside = (lane >= q * sub) & (lane < (q + 1) * sub)
                    row = jnp.where(inside, turned[q][j : j + 1], row)
            hop_rows[c, k : k + 1, :] = row

    slot = lax.broadcasted_iota(jnp.int32, (LANES, LANES), 0)

    def build(o, carry):
        start = pl.multiple_of(o * LANES, LANES)
        place = slot + o * LANES
        for c in range(chunks):
            columns = slice(c * LANES, (c + 1) * LANES)
            count = jnp.zeros((LANES, LANES), F32)
            for k in range(fan2):
                count = count + jnp.where(hop_rows[c, k : k + 1, :] == place, 1.0, 0.0)
            pick_two[pl.ds(start, LANES), columns] = count.astype(BF16)
            pick_one[pl.ds(start, LANES), columns] = jnp.where(
                hop_rows[c, fan2 : fan2 + 1, :] == place, 1.0, 0.0
            ).astype(BF16)
        return carry

    half = nd // 2
    lax.fori_loop(0, half, build, 0)

    for copy in serves:
        copy.wait_recv()
    everyone_copies = [
        remote(back, everyone.at[mf], all_send.at[d], all_recv.at[d], {"feat": feat_at(d)})
        for d in range(1, nf)
    ]
    everyone[mf] = back[...]

    lax.fori_loop(half, nd, build, 0)

    for copy in early:
        copy.wait_recv()
    w2_full[...] = jnp.concatenate(
        [w2_all[f, :, :hid_dev] for f in range(nf)]
        + [w2_all[f, :, hid_dev : 2 * hid_dev] for f in range(nf)],
        axis=1,
    )
    turned = [
        jnp.transpose(jnp.broadcast_to(bias_all[f], (LANES, bias_all.shape[2]))) for f in range(nf)
    ]
    b1 = jnp.concatenate([t[:hid_dev] for t in turned], axis=0)
    b2 = jnp.concatenate([t[hid_dev : 2 * hid_dev] for t in turned], axis=0)
    for copy in seed_copies:
        copy.wait_recv()
    if height % 16:
        x_seed = seed_all[...].astype(F32).reshape(depth, LANES)
    else:
        x_seed = seed_all[...].reshape(depth, LANES).astype(F32)
    x_seed = pltpu.roll(x_seed, lax.rem(2 * LANES - sub - within, LANES), 1)

    for copy in everyone_copies:
        copy.wait_recv()
    for o in range(nd):
        live = lane < live_ref[0, o]
        if height % 16:
            block = everyone[:, o].astype(F32).reshape(depth, LANES)
        else:
            block = everyone[:, o].reshape(depth, LANES).astype(F32)
        fetched[:, o * LANES : (o + 1) * LANES] = jnp.where(live, block, 0.0).astype(BF16)

    wide = 2 * LANES
    total = jnp.zeros((depth, LANES), F32)
    for n in range(chunks * LANES // wide):
        columns = slice(n * wide, (n + 1) * wide)
        own = jnp.dot(fetched[...], pick_one[:, columns], preferred_element_type=F32)
        mean = jnp.dot(fetched[...], pick_two[:, columns], preferred_element_type=F32)
        total = total + own[:, :LANES] + own[:, LANES:]
        x_all[:, columns] = own.astype(BF16)
        m_all[:, columns] = (mean * (1.0 / fan2)).astype(BF16)

    def fold(value):
        width = sub
        while width < LANES:
            value = value + pltpu.roll(value, width, 1)
            width *= 2
        return value

    is_seed = lane >= LANES - sub
    last = slice((chunks - 1) * LANES, chunks * LANES)
    m_one = fold(total) * (1.0 / fan1)
    x_all[:, last] = jnp.where(is_seed, x_seed, x_all[:, last].astype(F32)).astype(BF16)
    m_all[:, last] = jnp.where(is_seed, m_one, m_all[:, last].astype(F32)).astype(BF16)

    total = jnp.zeros((hid, LANES), F32)
    for n in range(chunks * LANES // wide):
        columns = slice(n * wide, (n + 1) * wide)
        pre = jnp.dot(w1s_ref[...], x_all[:, columns], preferred_element_type=F32)
        pre = pre + jnp.dot(w1n_ref[...], m_all[:, columns], preferred_element_type=F32)
        left = jnp.maximum(pre[:, :LANES] + b1, 0.0)
        right = jnp.maximum(pre[:, LANES:] + b1, 0.0)
        if n == chunks * LANES // wide - 1:
            h_seed = right
            right = jnp.where(is_seed, 0.0, right)
        total = total + left + right
    g_mean = fold(total) * (1.0 / fan1)
    stacked = jnp.concatenate([h_seed, g_mean], axis=0)
    z = jnp.zeros((hid, LANES), F32)
    for term in reversed(split_three(stacked)):
        z = z + jnp.dot(w2_full[...], term, preferred_element_type=F32)
    z = z + b2
    square = jnp.sum(z * z, axis=0, keepdims=True)
    z = z * lax.rsqrt(square * (1.0 / hid) + 1.0)
    for f in range(nf):
        z_own[f] = z[f * hid_dev : (f + 1) * hid_dev]

    z_copies = [
        remote(
            z_own.at[feat_at(d)],
            z_all.at[mf],
            z_send.at[d],
            z_recv.at[d],
            {"feat": feat_at(d)},
        )
        for d in range(1, nf)
    ]
    z_all[mf] = z_own[mf]
    for copy in wants + early + seed_copies + serves + everyone_copies:
        copy.wait_send()
    for copy in z_copies:
        copy.wait_recv()
    for g in range(groups):
        block = jnp.zeros((hid_dev, LANES), F32)
        for q in range(per):
            value = z_all[g * per + q]
            shift = (q * sub + sub) % LANES
            if shift:
                value = pltpu.roll(value, shift, 1)
            inside = (lane >= q * sub) & (lane < (q + 1) * sub)
            block = jnp.where(inside, value, block)
        out_ref[:, g * LANES : (g + 1) * LANES] = block
    for copy in z_copies:
        copy.wait_send()


def per_device(
    nd,
    nf,
    features,
    seed_rows,
    want_rows,
    live_counts,
    hop_one,
    hop_two,
    w1_self,
    w1_neigh,
    b1,
    w2_self,
    w2_neigh,
    b2,
):
    height, nodes = features.shape
    seeds = seed_rows.shape[0]
    hid_dev = b1.shape[0]
    hid, depth = w1_self.shape
    cap = want_rows.shape[2]
    fan1 = hop_one.shape[0]
    fan2 = hop_two.shape[0]
    columns = (fan1 + 1) * (seeds // nf)
    w2 = jnp.concatenate([w2_self, w2_neigh], axis=1)
    bias = jnp.concatenate([b1, b2]).reshape(1, 2 * hid_dev)
    vmem = pl.BlockSpec(memory_space=pltpu.VMEM)
    dma = pltpu.SemaphoreType.DMA
    return pl.pallas_call(
        functools.partial(kernel, nd, nf),
        out_shape=jax.ShapeDtypeStruct((hid_dev, seeds), F32),
        in_specs=[
            pl.BlockSpec(memory_space=pl.ANY),
            vmem,
            vmem,
            pl.BlockSpec(memory_space=pltpu.SMEM),
        ]
        + [vmem] * 6,
        out_specs=vmem,
        scratch_shapes=[
            pltpu.VMEM((height, nodes), BF16),
            pltpu.VMEM((nd, nd, cap), jnp.int32),
            pltpu.VMEM((nd, height, cap), BF16),
            pltpu.VMEM((nd, height, cap), BF16),
            pltpu.VMEM((nf, nd, height, cap), BF16),
            pltpu.VMEM((seeds // LANES, height, LANES), BF16),
            pltpu.VMEM((nf, height, LANES), BF16),
            pltpu.VMEM((nf, hid, 2 * hid_dev), BF16),
            pltpu.VMEM((nf, 1, 2 * hid_dev), F32),
            pltpu.VMEM((columns // LANES, 16, LANES), jnp.int32),
            pltpu.VMEM((nd * cap, columns), BF16),
            pltpu.VMEM((nd * cap, columns), BF16),
            pltpu.VMEM((depth, nd * cap), BF16),
            pltpu.VMEM((depth, columns), BF16),
            pltpu.VMEM((depth, columns), BF16),
            pltpu.VMEM((hid, 2 * hid), BF16),
            pltpu.VMEM((nf, hid_dev, LANES), F32),
            pltpu.VMEM((nf, hid_dev, LANES), F32),
            dma,
        ]
        + [dma((nd,))] * 4
        + [dma((nf,))] * 10,
        compiler_params=pltpu.CompilerParams(collective_id=0, has_side_effects=True),
    )(
        features,
        seed_rows.reshape(1, seeds),
        want_rows,
        live_counts,
        hop_one,
        hop_two,
        w1_self,
        w1_neigh,
        w2,
        bias,
    )


def solution(mesh):
    return jax.shard_map(
        functools.partial(per_device, mesh.shape["dom"], mesh.shape["feat"]),
        mesh=mesh,
        in_specs=(
            P("feat", "dom"),
            P("dom"),
            P("dom", None, None),
            P("dom", None),
            P(None, "dom"),
            P(None, None, "dom"),
            P(),
            P(),
            P("feat"),
            P(None, "feat"),
            P(None, "feat"),
            P("feat"),
        ),
        out_specs=P("feat", "dom"),
        check_vma=False,
    )
```

time: 155 us -> 40.5 us (0.26)
  waiting for transfers between devices: 77.9 us -> 0 us
  Pallas kernels: 0 us -> 36.3 us
  matrix products: 22 us -> 0 us
  local copies, waits for them, and re-layouts: 17.9 us -> 2.48 us
  between operations: 13.4 us -> 0.04 us
  starting transfers between devices: 9.84 us -> 0 us
  blocking collectives: 8.85 us -> 0 us
  other arithmetic: 4.35 us -> 1.39 us
    all_gather x2 -> x0, waiting for transfers between devices: 53.9 us -> none  [the longest x1 27.4 us: per_device(): lax.all_gather(means, 'feat', axis=0, tiled=True)]
    pallas_call x0 -> x1, Pallas kernels: none -> 36.3 us  [per_device(): pl.pallas_call(functools.partial(kernel, nd, nf), out_shape=jax.ShapeDtyp...]
    dot_general x8 -> x0, matrix products: 22 us -> none  [the longest x2 15.4 us: add_block(): jnp.dot(piece, pick_two, preferred_element_type=jnp.float32)]
    unnamed x4 -> x0, waiting for transfers between devices: 19.6 us -> none
    all_to_all x2 -> x0, starting transfers between devices: 9.54 us -> none  [the longest x1 5.34 us: per_device(): lax.all_to_all(want_rows, 'dom', split_axis=1, concat_axis=0, tiled=True)]
    gather x3 -> x0, local copies, waits for them, and re-layouts: 9.19 us -> none  [the longest x2 5.73 us: per_device(): jnp.take(features, lax.all_to_all(want_rows, 'dom', split_axis=1, concat_...]
    psum x1 -> x0, blocking collectives: 8.85 us -> none  [per_device(): square = lax.psum(jnp.sum(z_out * z_out, axis=0), 'feat')]
    all_to_all x2 -> x0, waiting for transfers between devices: 4.41 us -> none  [the longest x1 4.41 us: per_device(): lax.all_to_all(served, 'dom', split_axis=1, concat_axis=1, tiled=True)]
  transfers between devices with their start and end apart: 5 -> 0, of which waited for: 4 -> 0; matrix products, arithmetic and copies ran while one was open for 8% -> 0% of each run, Pallas kernels for 0% -> 0%
where the time goes in v1:
time: 40.5 us; the launch traced here: 40.2 us
  Pallas kernels  36.3 us (90%)
  local copies, waits for them, and re-layouts  2.48 us (6%)
  other arithmetic  1.39 us (3%)
    pallas_call x1, Pallas kernels, per_device(): pl.pallas_call(functools.partial(kernel, nd, nf), out_shape=jax.ShapeDtyp...  36.3 us
    unnamed x9, local copies, waits for them, and re-layouts  2.48 us

profile of v1, /device:TPU:0, one launch (start us, length us, event | category | flops | bytes accessed | tf_op | source)
XLA Modules:
  0.0 40.2 jit_solution(15846963753819116280)
XLA Ops:
  0.0 0.0 copy-start
  0.0 0.9 %copy.13 = bf16[256,64]{1,0:T(8,128)(2,1)S(1)} copy(bf16[256,64]{0,1:T(8,128)(2,1)} %param.21) | data formatting | bytes 65536 | tf_op args[9]
  0.9 0.0 copy-done
  0.9 0.1 copy.14
  1.0 0.0 copy-start.1
  1.0 0.0 copy-start.2
  1.0 0.7 %pad_maximum_fusion.w2_ref = bf16[256,128]{1,0:T(8,128)(2,1)} fusion(bf16[256,64]{1,0:T(8,128)(2,1)S(1)} %copy.14, bf16[256,64]{1,0:T(8,128)(2,1)S(1)} %copy.13), kind=kLoop, calls=%fused_computation | loop fusion | flops 131072 | bytes 131072 | tf_op jit(solution)/shard_map/concatenate | solution.py:369
  1.8 0.0 copy-done.1
  1.8 0.0 copy-done.2
  1.8 0.7 %maximum_bitcast_fusion.bias_ref = f32[1,128]{1,0:T(1,128)} fusion(f32[64]{0:T(128)S(1)} %copy-done.1, f32[64]{0:T(128)S(1)} %copy-done.2), kind=kLoop, calls=%fused_computation.1 | loop fusion | flops 128 | bytes 1024 | tf_op jit(solution)/shard_map/reshape | solution.py:370
  2.4 36.3 %shard_map.118 = f32[64,256]{1,0:T(8,128)} custom-call(bf16[32,16384]{1,0:T(8,128)(2,1)} %feat_hbm.1, s32[1,256]{1,0:T(1,128)} %bitcast.3, s32[1,8,128]{2,1,0:T(8,128)} %want_ref.1, s32[1,8]{1,0:T(1,128)} %live_ref.1, s32[15,256]{1,0:T(8,128)} %one_ref.1, s32[10,15,256]{2,1,0:T(8,128)} %two_ref.1, bf16[256,128]{1,0:T(8,128)(2,1)} %w1s_ref.1, ...), custom_call_target="tpu_custom_call" | custom-call | tf_op jit(solution)/shard_map/pallas_call | solution.py:373
  38.7 1.5 %copy.16 = f32[64,256]{1,0:T(8,128)} copy(f32[64,256]{1,0:T(8,128)} %shard_map.118) | data formatting | bytes 131072
Async XLA Ops:
  0.0 0.9 %copy-start = (bf16[256,64]{0,1:T(8,128)(2,1)S(1)}, bf16[256,64]{0,1:T(8,128)(2,1)}, u32[]{:S(2)}) copy-start(bf16[256,64]{0,1:T(8,128)(2,1)} %param.22) | copy-start | bytes 98308
  1.0 0.8 %copy-start.1 = (f32[64]{0:T(128)S(1)}, f32[64]{0:T(128)}, u32[]{:S(2)}) copy-start(f32[64]{0:T(128)} %param.23) | copy-start | bytes 772
  1.0 0.7 %copy-start.2 = (f32[64]{0:T(128)S(1)}, f32[64]{0:T(128)}, u32[]{:S(2)}) copy-start(f32[64]{0:T(128)} %param.20) | copy-start | bytes 772

commit v2 on v1

--- a/solution.py
+++ b/solution.py
@@ -18,7 +18,7 @@
     shape = (height, LANES)
     high = [jnp.broadcast_to(r >> 7, shape) for r in rows]
     low = [jnp.broadcast_to(r & (LANES - 1), shape) for r in rows]
-    step = 4
+    step = min(32, nodes // LANES)
 
     def body(i, accs):
         for u in range(step):
@@ -58,8 +58,10 @@
     two_ref,
     w1s_ref,
     w1n_ref,
-    w2_ref,
-    bias_ref,
+    w2s_ref,
+    w2n_ref,
+    b1_ref,
+    b2_ref,
     out_ref,
     feat_vm,
     got,
@@ -69,7 +71,8 @@
     seed_own,
     seed_all,
     w2_all,
-    bias_all,
+    b1_all,
+    b2_all,
     hop_rows,
     pick_one,
     pick_two,
@@ -88,10 +91,8 @@
     all_recv,
     seed_send,
     seed_recv,
-    w2_send,
-    w2_recv,
-    bias_send,
-    bias_recv,
+    early_send,
+    early_recv,
     z_send,
     z_recv,
 ):
@@ -142,11 +143,20 @@
     early = []
     for d in range(1, nf):
         where = {"feat": feat_at(d)}
-        early.append(remote(bias_ref, bias_all.at[mf], bias_send.at[d], bias_recv.at[d], where))
-        early.append(remote(w2_ref, w2_all.at[mf], w2_send.at[d], w2_recv.at[d], where))
+        for i, (src, dst) in enumerate(
+            (
+                (b1_ref, b1_all.at[mf]),
+                (b2_ref, b2_all.at[mf]),
+                (w2s_ref, w2_all.at[0, mf]),
+                (w2n_ref, w2_all.at[1, mf]),
+            )
+        ):
+            early.append(remote(src, dst, early_send.at[d, i], early_recv.at[d, i], where))
     got[me] = want_ref[0]
-    bias_all[mf] = bias_ref[...]
-    w2_all[mf] = w2_ref[...]
+    b1_all[mf] = b1_ref[...]
+    b2_all[mf] = b2_ref[...]
+    w2_all[0, mf] = w2s_ref[...]
+    w2_all[1, mf] = w2n_ref[...]
 
     feat_copy.wait()
     groups = seeds // LANES
@@ -169,7 +179,28 @@
     for copy in wants:
         copy.wait_recv()
 
-    serves = []
+    def forward(part):
+        copies = []
+        for d in part:
+            source = lax.rem(me + nd - d, nd)
+            if d:
+                serves[d].wait_recv()
+            for e in range(1, nf):
+                copies.append(
+                    remote(
+                        back.at[source],
+                        everyone.at[mf, source],
+                        all_send.at[d, e],
+                        all_recv.at[d, e],
+                        {"feat": feat_at(e)},
+                    )
+                )
+            everyone[mf, source] = back[source]
+        return copies
+
+    serves = {}
+    everyone_copies = []
+    parts = []
     order = list(range(1, nd)) + [0]
     for first in range(0, nd, 4):
         part = order[first : first + 4]
@@ -179,15 +210,12 @@
                 back[me] = block.astype(BF16)
                 continue
             served[d] = block.astype(BF16)
-            serves.append(
-                remote(
-                    served.at[d],
-                    back.at[me],
-                    serve_send.at[d],
-                    serve_recv.at[d],
-                    {"dom": dom_at(d)},
-                )
+            serves[d] = remote(
+                served.at[d], back.at[me], serve_send.at[d], serve_recv.at[d], {"dom": dom_at(d)}
             )
+        if parts:
+            everyone_copies += forward(parts[-1])
+        parts.append(part)
 
     lane = lax.broadcasted_iota(jnp.int32, (1, LANES), 1)
     base = pl.multiple_of(mf * sub // LANES * LANES, LANES)
@@ -228,28 +256,21 @@
     half = nd // 2
     lax.fori_loop(0, half, build, 0)
 
-    for copy in serves:
-        copy.wait_recv()
-    everyone_copies = [
-        remote(back, everyone.at[mf], all_send.at[d], all_recv.at[d], {"feat": feat_at(d)})
-        for d in range(1, nf)
-    ]
-    everyone[mf] = back[...]
+    everyone_copies += forward(parts[-1])
 
     lax.fori_loop(half, nd, build, 0)
 
     for copy in early:
         copy.wait_recv()
-    w2_full[...] = jnp.concatenate(
-        [w2_all[f, :, :hid_dev] for f in range(nf)]
-        + [w2_all[f, :, hid_dev : 2 * hid_dev] for f in range(nf)],
-        axis=1,
-    )
-    turned = [
-        jnp.transpose(jnp.broadcast_to(bias_all[f], (LANES, bias_all.shape[2]))) for f in range(nf)
-    ]
-    b1 = jnp.concatenate([t[:hid_dev] for t in turned], axis=0)
-    b2 = jnp.concatenate([t[hid_dev : 2 * hid_dev] for t in turned], axis=0)
+    w2_full[...] = jnp.transpose(w2_all[...].reshape(2 * hid, w2_all.shape[3]))
+
+    def column(rows):
+        return jnp.concatenate(
+            [jnp.transpose(jnp.broadcast_to(rows[f], (LANES, hid_dev))) for f in range(nf)], axis=0
+        )
+
+    b1 = column(b1_all)
+    b2 = column(b2_all)
     for copy in seed_copies:
         copy.wait_recv()
     if height % 16:
@@ -310,8 +331,17 @@
     z = z + b2
     square = jnp.sum(z * z, axis=0, keepdims=True)
     z = z * lax.rsqrt(square * (1.0 / hid) + 1.0)
+    part_rows = hid_dev // per
     for f in range(nf):
-        z_own[f] = z[f * hid_dev : (f + 1) * hid_dev]
+        packed = jnp.zeros((part_rows, LANES), F32)
+        for p in range(per):
+            row = f * hid_dev + p * part_rows
+            value = z[row : row + part_rows]
+            shift = (p * sub + sub) % LANES
+            if shift:
+                value = pltpu.roll(value, shift, 1)
+            packed = jnp.where((lane >= p * sub) & (lane < (p + 1) * sub), value, packed)
+        z_own[f] = packed
 
     z_copies = [
         remote(
@@ -324,20 +354,21 @@
         for d in range(1, nf)
     ]
     z_all[mf] = z_own[mf]
-    for copy in wants + early + seed_copies + serves + everyone_copies:
+    for copy in wants + early + seed_copies + list(serves.values()) + everyone_copies:
         copy.wait_send()
     for copy in z_copies:
         copy.wait_recv()
     for g in range(groups):
-        block = jnp.zeros((hid_dev, LANES), F32)
-        for q in range(per):
-            value = z_all[g * per + q]
-            shift = (q * sub + sub) % LANES
-            if shift:
-                value = pltpu.roll(value, shift, 1)
-            inside = (lane >= q * sub) & (lane < (q + 1) * sub)
-            block = jnp.where(inside, value, block)
-        out_ref[:, g * LANES : (g + 1) * LANES] = block
+        for p in range(per):
+            block = jnp.zeros((part_rows, LANES), F32)
+            for q in range(per):
+                value = z_all[g * per + q]
+                shift = (q - p) * sub % LANES
+                if shift:
+                    value = pltpu.roll(value, shift, 1)
+                inside = (lane >= q * sub) & (lane < (q + 1) * sub)
+                block = jnp.where(inside, value, block)
+            out_ref[p * part_rows : (p + 1) * part_rows, g * LANES : (g + 1) * LANES] = block
     for copy in z_copies:
         copy.wait_send()
 
@@ -366,20 +397,18 @@
     fan1 = hop_one.shape[0]
     fan2 = hop_two.shape[0]
     columns = (fan1 + 1) * (seeds // nf)
-    w2 = jnp.concatenate([w2_self, w2_neigh], axis=1)
-    bias = jnp.concatenate([b1, b2]).reshape(1, 2 * hid_dev)
     vmem = pl.BlockSpec(memory_space=pltpu.VMEM)
     dma = pltpu.SemaphoreType.DMA
     return pl.pallas_call(
         functools.partial(kernel, nd, nf),
-        out_shape=jax.ShapeDtypeStruct((hid_dev, seeds), F32),
+        out_shape=pltpu.VMEM((hid_dev, seeds), F32),
         in_specs=[
             pl.BlockSpec(memory_space=pl.ANY),
             vmem,
             vmem,
             pl.BlockSpec(memory_space=pltpu.SMEM),
         ]
-        + [vmem] * 6,
+        + [vmem] * 8,
         out_specs=vmem,
         scratch_shapes=[
             pltpu.VMEM((height, nodes), BF16),
@@ -389,8 +418,9 @@
             pltpu.VMEM((nf, nd, height, cap), BF16),
             pltpu.VMEM((seeds // LANES, height, LANES), BF16),
             pltpu.VMEM((nf, height, LANES), BF16),
-            pltpu.VMEM((nf, hid, 2 * hid_dev), BF16),
-            pltpu.VMEM((nf, 1, 2 * hid_dev), F32),
+            pltpu.VMEM((2, nf, hid_dev, w2_self.shape[0]), BF16),
+            pltpu.VMEM((nf, 1, hid_dev), F32),
+            pltpu.VMEM((nf, 1, hid_dev), F32),
             pltpu.VMEM((columns // LANES, 16, LANES), jnp.int32),
             pltpu.VMEM((nd * cap, columns), BF16),
             pltpu.VMEM((nd * cap, columns), BF16),
@@ -398,12 +428,15 @@
             pltpu.VMEM((depth, columns), BF16),
             pltpu.VMEM((depth, columns), BF16),
             pltpu.VMEM((hid, 2 * hid), BF16),
-            pltpu.VMEM((nf, hid_dev, LANES), F32),
-            pltpu.VMEM((nf, hid_dev, LANES), F32),
+            pltpu.VMEM((nf, hid_dev * (seeds // nf) // LANES, LANES), F32),
+            pltpu.VMEM((nf, hid_dev * (seeds // nf) // LANES, LANES), F32),
             dma,
         ]
         + [dma((nd,))] * 4
-        + [dma((nf,))] * 10,
+        + [dma((nd, nf))] * 2
+        + [dma((nf,))] * 2
+        + [dma((nf, 4))] * 2
+        + [dma((nf,))] * 2,
         compiler_params=pltpu.CompilerParams(collective_id=0, has_side_effects=True),
     )(
         features,
@@ -414,8 +447,10 @@
         hop_two,
         w1_self,
         w1_neigh,
-        w2,
-        bias,
+        w2_self.T,
+        w2_neigh.T,
+        b1.reshape(1, hid_dev),
+        b2.reshape(1, hid_dev),
     )
 
 

time: 40.5 us -> 31 us (0.77)
  Pallas kernels: 36.3 us -> 30.2 us
  local copies, waits for them, and re-layouts: 2.48 us -> 0.63 us
  other arithmetic: 1.39 us -> 0 us
    pallas_call x1, Pallas kernels: 36.3 us -> 30.2 us  [per_device(): pl.pallas_call(functools.partial(kernel, nd, nf), out_shape=pltpu.VMEM((h...]
    unnamed x9 -> x1, local copies, waits for them, and re-layouts: 2.48 us -> 0.63 us
    concatenate x1 -> x0, other arithmetic: 0.72 us -> none  [per_device(): w2 = jnp.concatenate([w2_self, w2_neigh], axis=1)]
    reshape x1 -> x0, other arithmetic: 0.66 us -> none  [per_device(): bias = jnp.concatenate([b1, b2]).reshape(1, 2 * hid_dev)]
where the time goes in v2:
time: 31 us; the launch traced here: 30.9 us
  Pallas kernels  30.2 us (97%)
  local copies, waits for them, and re-layouts  0.63 us (2%)
    pallas_call x1, Pallas kernels, per_device(): pl.pallas_call(functools.partial(kernel, nd, nf), out_shape=pltpu.VMEM((h...  30.2 us
    unnamed x1, local copies, waits for them, and re-layouts  0.63 us

profile of v2, /device:TPU:0, one launch (start us, length us, event | category | flops | bytes accessed | tf_op | source)
XLA Modules:
  0.0 30.9 jit_solution(5611514508656950775)
XLA Ops:
  0.0 30.2 %shard_map.118 = f32[64,256]{1,0:T(8,128)S(1)} custom-call(bf16[32,16384]{1,0:T(8,128)(2,1)} %feat_hbm.1, s32[1,256]{1,0:T(1,128)} %bitcast.7, s32[1,8,128]{2,1,0:T(8,128)} %want_ref.1, s32[1,8]{1,0:T(1,128)} %live_ref.1, s32[15,256]{1,0:T(8,128)} %one_ref.1, s32[10,15,256]{2,1,0:T(8,128)} %two_ref.1, bf16[256,128]{1,0:T(8,128)(2,1)} %w1s_ref.1, ...), custom_call_target="tpu_custom_call" | custom-call | tf_op jit(solution)/shard_map/pallas_call | solution.py:402
  30.2 0.6 %copy.14 = f32[64,256]{1,0:T(8,128)} copy(f32[64,256]{1,0:T(8,128)S(1)} %shard_map.118) | data formatting | bytes 131072

commit v3 on v2

--- a/solution.py
+++ b/solution.py
@@ -54,16 +54,20 @@
     seed_ref,
     want_ref,
     live_ref,
-    one_ref,
-    two_ref,
-    w1s_ref,
-    w1n_ref,
+    one_hbm,
+    two_hbm,
+    w1s_hbm,
+    w1n_hbm,
     w2s_ref,
     w2n_ref,
     b1_ref,
     b2_ref,
     out_ref,
     feat_vm,
+    one_ref,
+    two_ref,
+    w1s_ref,
+    w1n_ref,
     got,
     served,
     back,
@@ -77,6 +81,8 @@
     pick_one,
     pick_two,
     fetched,
+    own_sum,
+    mean_sum,
     x_all,
     m_all,
     w2_full,
@@ -114,8 +120,18 @@
     def feat_at(d):
         return lax.rem(mf + d, nf)
 
-    feat_copy = pltpu.make_async_copy(feat_hbm, feat_vm, local_sem)
+    feat_copy = pltpu.make_async_copy(feat_hbm, feat_vm, local_sem.at[0])
     feat_copy.start()
+    hop_copies = [
+        pltpu.make_async_copy(one_hbm, one_ref, local_sem.at[1]),
+        pltpu.make_async_copy(two_hbm, two_ref, local_sem.at[2]),
+    ]
+    weight_copies = [
+        pltpu.make_async_copy(w1s_hbm, w1s_ref, local_sem.at[3]),
+        pltpu.make_async_copy(w1n_hbm, w1n_ref, local_sem.at[4]),
+        pltpu.make_async_copy(w2s_ref, w2_all.at[0, mf], local_sem.at[5]),
+        pltpu.make_async_copy(w2n_ref, w2_all.at[1, mf], local_sem.at[6]),
+    ]
 
     barrier = pltpu.get_barrier_semaphore()
     for d in range(1, nd):
@@ -155,8 +171,8 @@
     got[me] = want_ref[0]
     b1_all[mf] = b1_ref[...]
     b2_all[mf] = b2_ref[...]
-    w2_all[0, mf] = w2s_ref[...]
-    w2_all[1, mf] = w2n_ref[...]
+    for copy in hop_copies + weight_copies:
+        copy.start()
 
     feat_copy.wait()
     groups = seeds // LANES
@@ -199,11 +215,10 @@
         return copies
 
     serves = {}
-    everyone_copies = []
+    arrivals = []
     parts = []
     order = list(range(1, nd)) + [0]
-    for first in range(0, nd, 4):
-        part = order[first : first + 4]
+    for part in (order[: nd * 3 // 8], order[nd * 3 // 8 : nd * 6 // 8], order[nd * 6 // 8 :]):
         blocks = gather_columns(feat_vm, [got[dom_at(d), pl.ds(me, 1), :] for d in part])
         for d, block in zip(part, blocks):
             if d == 0:
@@ -214,12 +229,14 @@
                 served.at[d], back.at[me], serve_send.at[d], serve_recv.at[d], {"dom": dom_at(d)}
             )
         if parts:
-            everyone_copies += forward(parts[-1])
+            arrivals.append(forward(parts[-1]))
         parts.append(part)
 
     lane = lax.broadcasted_iota(jnp.int32, (1, LANES), 1)
     base = pl.multiple_of(mf * sub // LANES * LANES, LANES)
     within = lax.rem(mf * sub, LANES)
+    for copy in hop_copies:
+        copy.wait()
     for k in range(fan2 + 1):
         if k < fan2:
             rows = two_ref[k, :, pl.ds(base, LANES)]
@@ -241,7 +258,7 @@
 
     def build(o, carry):
         start = pl.multiple_of(o * LANES, LANES)
-        place = slot + o * LANES
+        place = slot + lax.rem(me + 2 * nd - 1 - o, nd) * LANES
         for c in range(chunks):
             columns = slice(c * LANES, (c + 1) * LANES)
             count = jnp.zeros((LANES, LANES), F32)
@@ -256,12 +273,15 @@
     half = nd // 2
     lax.fori_loop(0, half, build, 0)
 
-    everyone_copies += forward(parts[-1])
+    arrivals.append(forward(parts[-1]))
+    everyone_copies = [copy for part in arrivals for copy in part]
 
     lax.fori_loop(half, nd, build, 0)
 
     for copy in early:
         copy.wait_recv()
+    for copy in weight_copies:
+        copy.wait()
     w2_full[...] = jnp.transpose(w2_all[...].reshape(2 * hid, w2_all.shape[3]))
 
     def column(rows):
@@ -279,25 +299,37 @@
         x_seed = seed_all[...].reshape(depth, LANES).astype(F32)
     x_seed = pltpu.roll(x_seed, lax.rem(2 * LANES - sub - within, LANES), 1)
 
-    for copy in everyone_copies:
-        copy.wait_recv()
-    for o in range(nd):
-        live = lane < live_ref[0, o]
-        if height % 16:
-            block = everyone[:, o].astype(F32).reshape(depth, LANES)
-        else:
-            block = everyone[:, o].reshape(depth, LANES).astype(F32)
-        fetched[:, o * LANES : (o + 1) * LANES] = jnp.where(live, block, 0.0).astype(BF16)
-
     wide = 2 * LANES
     total = jnp.zeros((depth, LANES), F32)
-    for n in range(chunks * LANES // wide):
-        columns = slice(n * wide, (n + 1) * wide)
-        own = jnp.dot(fetched[...], pick_one[:, columns], preferred_element_type=F32)
-        mean = jnp.dot(fetched[...], pick_two[:, columns], preferred_element_type=F32)
-        total = total + own[:, :LANES] + own[:, LANES:]
-        x_all[:, columns] = own.astype(BF16)
-        m_all[:, columns] = (mean * (1.0 / fan2)).astype(BF16)
+    done = 0
+    for i, part in enumerate(parts):
+        for copy in arrivals[i]:
+            copy.wait_recv()
+        for d in part:
+            source = lax.rem(me + nd - d, nd)
+            live = lane < live_ref[0, source]
+            if height % 16:
+                block = everyone[:, source].astype(F32).reshape(depth, LANES)
+            else:
+                block = everyone[:, source].reshape(depth, LANES).astype(F32)
+            at = order.index(d) * LANES
+            fetched[:, at : at + LANES] = jnp.where(live, block, 0.0).astype(BF16)
+        these = slice(done, done + len(part) * LANES)
+        done += len(part) * LANES
+        for n in range(chunks * LANES // wide):
+            columns = slice(n * wide, (n + 1) * wide)
+            own = jnp.dot(fetched[:, these], pick_one[these, columns], preferred_element_type=F32)
+            mean = jnp.dot(fetched[:, these], pick_two[these, columns], preferred_element_type=F32)
+            if i:
+                own = own + own_sum[:, columns]
+                mean = mean + mean_sum[:, columns]
+            if i < len(parts) - 1:
+                own_sum[:, columns] = own
+                mean_sum[:, columns] = mean
+                continue
+            total = total + own[:, :LANES] + own[:, LANES:]
+            x_all[:, columns] = own.astype(BF16)
+            m_all[:, columns] = (mean * (1.0 / fan2)).astype(BF16)
 
     def fold(value):
         width = sub
@@ -408,10 +440,15 @@
             vmem,
             pl.BlockSpec(memory_space=pltpu.SMEM),
         ]
-        + [vmem] * 8,
+        + [pl.BlockSpec(memory_space=pl.ANY)] * 6
+        + [vmem] * 2,
         out_specs=vmem,
         scratch_shapes=[
             pltpu.VMEM((height, nodes), BF16),
+            pltpu.VMEM(hop_one.shape, jnp.int32),
+            pltpu.VMEM(hop_two.shape, jnp.int32),
+            pltpu.VMEM(w1_self.shape, BF16),
+            pltpu.VMEM(w1_neigh.shape, BF16),
             pltpu.VMEM((nd, nd, cap), jnp.int32),
             pltpu.VMEM((nd, height, cap), BF16),
             pltpu.VMEM((nd, height, cap), BF16),
@@ -425,12 +462,14 @@
             pltpu.VMEM((nd * cap, columns), BF16),
             pltpu.VMEM((nd * cap, columns), BF16),
             pltpu.VMEM((depth, nd * cap), BF16),
+            pltpu.VMEM((depth, columns), F32),
+            pltpu.VMEM((depth, columns), F32),
             pltpu.VMEM((depth, columns), BF16),
             pltpu.VMEM((depth, columns), BF16),
             pltpu.VMEM((hid, 2 * hid), BF16),
             pltpu.VMEM((nf, hid_dev * (seeds // nf) // LANES, LANES), F32),
             pltpu.VMEM((nf, hid_dev * (seeds // nf) // LANES, LANES), F32),
-            dma,
+            dma((7,)),
         ]
         + [dma((nd,))] * 4
         + [dma((nd, nf))] * 2

time: 31 us -> 30.2 us (0.974)
  Pallas kernels: 30.2 us -> 29.3 us
    pallas_call x1, Pallas kernels: 30.2 us -> 29.3 us  [per_device(): pl.pallas_call(functools.partial(kernel, nd, nf), out_shape=pltpu.VMEM((h...]
where the time goes in v3:
time: 30.2 us; the launch traced here: 30 us
  Pallas kernels  29.3 us (97%)
  local copies, waits for them, and re-layouts  0.63 us (2%)
    pallas_call x1, Pallas kernels, per_device(): pl.pallas_call(functools.partial(kernel, nd, nf), out_shape=pltpu.VMEM((h...  29.3 us
    unnamed x1, local copies, waits for them, and re-layouts  0.63 us

profile of v3, /device:TPU:0, one launch (start us, length us, event | category | flops | bytes accessed | tf_op | source)
XLA Modules:
  0.0 30.0 jit_solution(2480106891857820166)
XLA Ops:
  0.0 29.3 %shard_map.118 = f32[64,256]{1,0:T(8,128)S(1)} custom-call(bf16[32,16384]{1,0:T(8,128)(2,1)} %feat_hbm.1, s32[1,256]{1,0:T(1,128)} %bitcast.7, s32[1,8,128]{2,1,0:T(8,128)} %want_ref.1, s32[1,8]{1,0:T(1,128)} %live_ref.1, s32[15,256]{1,0:T(8,128)} %one_hbm.1, s32[10,15,256]{2,1,0:T(8,128)} %two_hbm.1, bf16[256,128]{1,0:T(8,128)(2,1)} %w1s_hbm.1, ...), custom_call_target="tpu_custom_call" | custom-call | tf_op jit(solution)/shard_map/pallas_call | solution.py:434
  29.3 0.6 %copy.14 = f32[64,256]{1,0:T(8,128)} copy(f32[64,256]{1,0:T(8,128)S(1)} %shard_map.118) | data formatting | bytes 131072
